TPU v7x, 32 devices: a whole 2x2x4 slice. The times are simulated.
32 devices in a mesh: groups: 2 (over x), seq: 16 (over z, y, core).
Axes of the slice: x: 2, y: 2, z: 4, core: 2. Of those that a mesh axis runs over, the one named last changes fastest.
Arguments:
- self_query: bfloat16 [16, 8192], P('groups'), parts along dimension 0, may hold values from -128 to 128
- new_key: bfloat16 [16, 8192], P('groups'), parts along dimension 0, may hold values from -6 to 6
- new_value: bfloat16 [16, 8192], P('groups'), parts along dimension 0, may hold values from -12 to 12
- cache_keys: bfloat16 [16, 1024, 8192], P('groups', 'seq'), parts along dimension 0, may hold values from -8 to 8
- cache_values: bfloat16 [16, 1024, 8192], P('groups', 'seq'), parts along dimension 0, may hold values from -12 to 12
- lengths: int32 [16], P('groups'), parts along dimension 0, may hold values from 128 to 1024
- db_keys: bfloat16 [32, 128, 8192], P(('groups', 'seq')), parts along dimension 0, may hold values from -8 to 8
- db_values: bfloat16 [32, 128, 8192], P(('groups', 'seq')), parts along dimension 0, may hold values from -12 to 12
- cross_query: bfloat16 [16, 8192], P('groups'), parts along dimension 0, may hold values from -128 to 128
- neighbour_ids: int32 [16, 2], P('groups'), parts along dimension 0, may hold values from 0 to 15
Outputs:
- self_out: bfloat16 [16, 8192], P('groups', 'seq'), parts along dimension 0
- cross_out: bfloat16 [16, 8192], P('groups', 'seq'), parts along dimension 0
There are 2 independent parts, one for each index of `groups`. A program takes and returns all parts, laid end to end along the dimension named above; each array names one. Nothing has to cross between parts.
Inputs may be any that keep to these rules, and one draw needn't show every extreme that they name: `neighbour_ids`: the 2 ids of a row may repeat.
All inputs are finite; a program needn't handle non-finite values.
Results may differ from a plain program's by a relative error of at most 0.022.
Values may be sent and summed in bfloat16 or wider, within the bound.
A program may use at most 64 MiB of HBM per device.

v0:
```python
import functools

import jax
import jax.numpy as jnp
from jax import lax
from jax.experimental import pallas as pl
from jax.experimental.pallas import tpu as pltpu
from jax.sharding import PartitionSpec as P

DH = 128
NEG = -1e30
FLOOR = -1e29
MESH = pl.DeviceIdType.MESH


def offset_of(step, count):
    return count // 2 + ((step + 1) // 2) * (1 - 2 * (step % 2))


def spread_queries(block, first, total):
    rows, width = block.shape
    zero = jnp.zeros((rows, DH), block.dtype)
    heads = width // DH
    return jnp.concatenate(
        [
            jnp.concatenate(
                [
                    block[:, h * DH : (h + 1) * DH] if first + h == i else zero
                    for h in range(heads)
                ],
                axis=1,
            )
            for i in range(total)
        ],
        axis=0,
    ).astype(jnp.bfloat16)


def weigh(queries, keys, bias, counts):
    scores = sum(
        lax.dot_general(k, q, (((1,), (1,)), ((), ())), preferred_element_type=jnp.float32)
        for q, k in zip(queries, keys)
    )
    scores = scores.T * (DH ** (-0.5)) + jnp.concatenate([bias] * (scores.shape[1] // bias.shape[0]))
    peak = jnp.maximum(jnp.max(scores, axis=1, keepdims=True), FLOOR)
    weights = jnp.exp(scores - peak)
    if counts is not None:
        weights = weights * jnp.concatenate([counts] * (scores.shape[0] // counts.shape[0]))
    den = jnp.maximum(jnp.sum(weights, axis=1, keepdims=True), 0.5)
    return weights.astype(jnp.bfloat16), 1.0 / den, peak + jnp.log(den)


def kernel(
    parts,
    ahead,
    lengths_in,
    ids_in,
    self_query,
    new_key,
    new_value,
    cache_keys,
    cache_values,
    db_keys,
    db_values,
    cross_query,
    out,
    lengths,
    ids,
    keys,
    values,
    dkeys,
    dvalues,
    squery,
    cquery,
    nkey,
    nvalue,
    bias,
    cbias,
    ccounts,
    outbox,
    sidebox,
    merged,
    inbox,
    stats,
    stream_sem,
    small_sem,
    send_sem,
    recv_sem,
    side_send,
    side_recv,
):
    me = lax.axis_index("seq")
    rows, positions, width = cache_keys.shape
    entries, tokens, _ = db_keys.shape
    span = width // parts
    pairs = span // (2 * DH)
    columns = 2 * pairs

    chips = parts // 2
    core = lax.rem(me, 2)
    chip = me // 2
    partner = chip * 2 + 1 - core

    def peer(step):
        return lax.rem(chip + offset_of(step, chips), chips) * 2 + core

    def target(k):
        flip = 1 - lax.rem(k, 2)
        return peer(k // 2) - core + core * (1 - flip) + (1 - core) * flip

    def lanes_of(device):
        return pl.ds(pl.multiple_of(device * span, span), span)

    def streams(step):
        lanes = lanes_of(target(step))
        return [
            pltpu.make_async_copy(source.at[:, :, lanes], dest.at[step], stream_sem.at[k, step])
            for k, (source, dest) in enumerate(
                (
                    (cache_keys, keys),
                    (cache_values, values),
                    (db_keys, dkeys),
                    (db_values, dvalues),
                )
            )
        ]

    def handover(step):
        return pltpu.make_async_remote_copy(
            src_ref=outbox.at[2 * step],
            dst_ref=sidebox.at[step],
            send_sem=side_send.at[step],
            recv_sem=side_recv.at[step],
            device_id={"seq": partner},
            device_id_type=MESH,
        )

    def message(step):
        return pltpu.make_async_remote_copy(
            src_ref=merged.at[step],
            dst_ref=inbox.at[step],
            send_sem=send_sem.at[step],
            recv_sem=recv_sem.at[step],
            device_id={"seq": peer(step)},
            device_id_type=MESH,
        )

    own = lanes_of(me)
    small = [
        pltpu.make_async_copy(self_query, squery, small_sem.at[0]),
        pltpu.make_async_copy(cross_query, cquery, small_sem.at[1]),
        pltpu.make_async_copy(new_key.at[:, own], nkey, small_sem.at[2]),
        pltpu.make_async_copy(new_value.at[:, own], nvalue, small_sem.at[3]),
    ]
    scalars = [
        pltpu.make_async_copy(lengths_in, lengths, small_sem.at[4]),
        pltpu.make_async_copy(ids_in, ids, small_sem.at[5]),
    ]
    for copy in small[:2] + scalars:
        copy.start()

    def launch(step, carry):
        for copy in streams(step):
            copy.start()
        return carry

    lax.fori_loop(0, 2 * ahead, launch, 0)
    small[2].start()
    small[3].start()

    barrier = pltpu.get_barrier_semaphore()

    def greet(step, carry):
        pl.semaphore_signal(
            barrier, inc=1, device_id={"seq": peer(step)}, device_id_type=MESH
        )
        return carry

    lax.fori_loop(0, chips - 1, greet, 0)
    pl.semaphore_signal(barrier, inc=1, device_id={"seq": partner}, device_id_type=MESH)

    for copy in scalars:
        copy.wait()
    shape = (2 * rows, rows * positions)
    row = lax.broadcasted_iota(jnp.int32, shape, 0)
    row = jnp.where(row >= rows, row - rows, row)
    lane = lax.broadcasted_iota(jnp.int32, shape, 1)
    table = jnp.full(shape, NEG, jnp.float32)
    for b in range(rows):
        left = jnp.clip(lengths[b] - me * positions, 0, positions)
        live = (row == b) & (lane >= b * positions) & (lane < b * positions + left)
        table = jnp.where(live, 0.0, table)
    bias[...] = table
    shape = (2 * rows, entries * tokens)
    row = lax.broadcasted_iota(jnp.int32, shape, 0)
    row = jnp.where(row >= rows, row - rows, row)
    lane = lax.broadcasted_iota(jnp.int32, shape, 1)
    table = jnp.zeros(shape, jnp.float32)
    for b in range(rows):
        for e in range(entries):
            here = (row == b) & (lane >= e * tokens) & (lane < (e + 1) * tokens)
            for j in range(ids.shape[0]):
                match = here & (jnp.full(shape, ids[j, b], jnp.int32) == me * entries + e)
                table = jnp.where(match, table + 1.0, table)
    ccounts[...] = table
    cbias[...] = jnp.where(table > 0.0, 0.0, NEG)

    small[0].wait()
    small[1].wait()
    tag = lax.broadcasted_iota(jnp.int32, (2 * rows, DH), 1)

    def compute_both(first):
        heads = 2 * pairs
        results = []
        for source, held, extent, table, number in (
            (squery, keys, rows * positions, bias[...], None),
            (cquery, dkeys, entries * tokens, cbias[...], ccounts[...]),
        ):
            queries, blocks = [], []
            for j in range(2):
                lanes = lanes_of(target(first + j))
                block = source[:, lanes].astype(jnp.float32)
                queries.append(spread_queries(block, j * heads, 2 * heads))
                blocks.append(held[first + j].reshape(extent, span))
            results.append(weigh(queries, blocks, table, number))
        for j in range(2):
            compute(first + j, j, results)

    def compute(step, place, results):
        found = [None] * columns
        sums = []
        for pair in range(pairs):
            piece = slice(pair * 2 * DH, (pair + 1) * 2 * DH)
            at = slice((place * pairs + pair) * 2 * rows, (place * pairs + pair + 1) * 2 * rows)
            accs = []
            for kind, (held, extent) in enumerate(
                ((values, rows * positions), (dvalues, entries * tokens))
            ):
                weights, inverse, level = results[kind]
                acc = jnp.dot(
                    weights[at],
                    held[step, :, :, piece].reshape(extent, 2 * DH),
                    preferred_element_type=jnp.float32,
                )
                accs.append(acc * inverse[at])
                found[kind * pairs + pair] = level[at]
            acc, cacc = accs
            sums.append(jnp.concatenate([acc[:rows, :DH], cacc[:rows, :DH]], axis=0))
            sums.append(jnp.concatenate([acc[rows:, DH:], cacc[rows:, DH:]], axis=0))
        for head, part in enumerate(sums):
            outbox[step, :, head * DH : (head + 1) * DH] = part.astype(jnp.bfloat16)
        level = jnp.zeros((2 * rows, DH), jnp.float32)
        for k in range(3 * columns):
            level = jnp.where(tag == k, found[k % columns], level)
        outbox[step, :, span:] = packed(level)

    def spread(tile, head):
        pair, half = head // 2, head % 2
        part = tile[half * rows : (half + 1) * rows]
        return jnp.concatenate(
            [
                jnp.broadcast_to(part[:, pair : pair + 1], (rows, DH)),
                jnp.broadcast_to(part[:, pairs + pair : pairs + pair + 1], (rows, DH)),
            ],
            axis=0,
        )

    def level_of(box, step):
        raw = box[step, :, span:].astype(jnp.float32)
        full = raw + pltpu.roll(raw, DH - columns, 1) + pltpu.roll(raw, DH - 2 * columns, 1)
        return jnp.where(tag < columns, full, NEG)

    def packed(level):
        high = level.astype(jnp.bfloat16).astype(jnp.float32)
        rest = level - high
        middle = rest.astype(jnp.bfloat16).astype(jnp.float32)
        low = rest - middle
        level = jnp.where(tag < columns, high, jnp.where(tag < 2 * columns, middle, low))
        return level.astype(jnp.bfloat16)

    def merge(step):
        first, second = level_of(outbox, 2 * step + 1), level_of(sidebox, step)
        top = jnp.maximum(first, second)
        share, other = jnp.exp(first - top), jnp.exp(second - top)
        total = share + other
        inverse = 1.0 / total
        share, other = share * inverse, other * inverse
        for h in range(2 * pairs):
            piece = slice(h * DH, (h + 1) * DH)
            part = outbox[2 * step + 1, :, piece].astype(jnp.float32) * spread(share, h)
            part = part + sidebox[step, :, piece].astype(jnp.float32) * spread(other, h)
            merged[step, :, piece] = part.astype(jnp.bfloat16)
        level = top + jnp.log(total)
        level = jnp.where(tag < columns, level, 0.0)
        level = (
            level
            + jnp.where(tag < 2 * columns, pltpu.roll(level, columns, 1), 0.0)
            + pltpu.roll(level, 2 * columns, 1)
        )
        merged[step, :, span:] = packed(level)

    def block(step, fill):
        for j in range(2):
            for copy in streams(2 * step + j):
                copy.wait()
        if fill:
            for j in range(2):
                for copy in streams(2 * (step + ahead) + j):
                    copy.start()
        compute_both(2 * step)
        handover(step).start()

    def pass_on(step):
        handover(step).wait_recv()
        merge(step)
        message(step).start()

    pl.semaphore_wait(barrier, chips)
    block(0, ahead < chips)

    def turn(fill, step, carry):
        block(step, fill)
        pass_on(step - 1)
        return carry

    lax.fori_loop(1, chips - ahead, functools.partial(turn, True), 0)
    lax.fori_loop(max(1, chips - ahead), chips, functools.partial(turn, False), 0)

    small[2].wait()
    small[3].wait()
    query_own = squery[:, own].astype(jnp.float32)
    product = query_own * nkey[...].astype(jnp.float32)
    level_own = jnp.full((2 * rows, DH), NEG, jnp.float32)
    for pair in range(pairs):
        halves = [
            jnp.sum(product[:, h * DH : (h + 1) * DH], axis=1, keepdims=True) * (DH ** (-0.5))
            for h in (2 * pair, 2 * pair + 1)
        ]
        level_own = jnp.where(tag == pair, jnp.concatenate(halves, axis=0), level_own)

    boxes = [(outbox, parts - 1)] + [(inbox, step) for step in range(chips - 2)]
    boxes += [(sidebox, chips - 1), (inbox, chips - 2)]
    top = level_own
    for k, (box, step) in enumerate(boxes):
        if box is inbox:
            message(step).wait_recv()
        if box is sidebox:
            handover(step).wait_recv()
        level = level_of(box, step)
        stats[k] = level
        top = jnp.maximum(top, level)
    share = jnp.exp(level_own - top)
    total = share
    zero = jnp.zeros((rows, DH), jnp.float32)
    sums = [
        jnp.concatenate([nvalue[:, h * DH : (h + 1) * DH].astype(jnp.float32), zero], axis=0)
        * spread(share, h)
        for h in range(2 * pairs)
    ]
    for k, (box, step) in enumerate(boxes):
        share = jnp.exp(stats[k] - top)
        total = total + share
        for h in range(2 * pairs):
            part = box[step, :, h * DH : (h + 1) * DH].astype(jnp.float32)
            sums[h] = sums[h] + part * spread(share, h)
    inverse = 1.0 / total
    for h in range(2 * pairs):
        result = sums[h] * spread(inverse, h)
        out[:, h * DH : (h + 1) * DH] = result.astype(jnp.bfloat16)

    def drain(step, carry):
        message(step).wait_send()
        return carry

    lax.fori_loop(0, chips - 1, drain, 0)

    def drain_side(step, carry):
        handover(step).wait_send()
        return carry

    lax.fori_loop(0, chips, drain_side, 0)


def on_device(
    self_query,
    new_key,
    new_value,
    cache_keys,
    cache_values,
    lengths,
    db_keys,
    db_values,
    cross_query,
    neighbour_ids,
):
    parts = lax.axis_size("seq")
    rows, positions, width = cache_keys.shape
    entries, tokens, _ = db_keys.shape
    span = width // parts
    chips = parts // 2
    ahead = min(3, chips)
    half = jnp.bfloat16
    anywhere = pl.BlockSpec(memory_space=pl.ANY)
    vmem = pl.BlockSpec(memory_space=pltpu.VMEM)
    out = pl.pallas_call(
        functools.partial(kernel, parts, ahead),
        out_shape=jax.ShapeDtypeStruct((2 * rows, span), half),
        in_specs=[anywhere] * 10,
        out_specs=vmem,
        scratch_shapes=[
            pltpu.SMEM(lengths.shape, jnp.int32),
            pltpu.SMEM(neighbour_ids.shape[::-1], jnp.int32),
            pltpu.VMEM((parts, rows, positions, span), half),
            pltpu.VMEM((parts, rows, positions, span), half),
            pltpu.VMEM((parts, entries, tokens, span), half),
            pltpu.VMEM((parts, entries, tokens, span), half),
            pltpu.VMEM((rows, width), half),
            pltpu.VMEM((rows, width), half),
            pltpu.VMEM((rows, span), half),
            pltpu.VMEM((rows, span), half),
            pltpu.VMEM((2 * rows, rows * positions), jnp.float32),
            pltpu.VMEM((2 * rows, entries * tokens), jnp.float32),
            pltpu.VMEM((2 * rows, entries * tokens), jnp.float32),
            pltpu.VMEM((parts, 2 * rows, span + DH), half),
            pltpu.VMEM((chips, 2 * rows, span + DH), half),
            pltpu.VMEM((chips, 2 * rows, span + DH), half),
            pltpu.VMEM((chips, 2 * rows, span + DH), half),
            pltpu.VMEM((chips + 1, 2 * rows, DH), jnp.float32),
            pltpu.SemaphoreType.DMA((4, parts)),
            pltpu.SemaphoreType.DMA((6,)),
            pltpu.SemaphoreType.DMA((chips,)),
            pltpu.SemaphoreType.DMA((chips,)),
            pltpu.SemaphoreType.DMA((chips,)),
            pltpu.SemaphoreType.DMA((chips,)),
        ],
        compiler_params=pltpu.CompilerParams(
            collective_id=0, has_side_effects=True, vmem_limit_bytes=60 * 1024 * 1024
        ),
    )(
        lengths,
        neighbour_ids.T,
        self_query,
        new_key,
        new_value,
        cache_keys,
        cache_values,
        db_keys,
        db_values,
        cross_query,
    )
    return out[:rows], out[rows:]


def solution(mesh):
    in_specs = (
        P("groups", None),
        P("groups", None),
        P("groups", None),
        P("groups", "seq", None),
        P("groups", "seq", None),
        P("groups"),
        P(("groups", "seq"), None, None),
        P(("groups", "seq"), None, None),
        P("groups", None),
        P("groups", None),
    )
    out_specs = (P("groups", "seq"), P("groups", "seq"))
    return jax.shard_map(
        on_device, mesh=mesh, in_specs=in_specs, out_specs=out_specs, check_vma=False
    )
```

profile of v0, /device:TPU:0, one launch (start us, length us, event | category | flops | bytes accessed | tf_op | source)
XLA Modules:
  0.0 24.1 jit_solution(12774421534255000268)
XLA Ops:
  0.6 22.2 %shard_map.113 = bf16[16,512]{1,0:T(8,128)(2,1)} custom-call(s32[8]{0:T(128)} %lengths_in.1, s32[2,8]{1,0:T(2,128)} %bitcast.1, bf16[8,8192]{1,0:T(8,128)(2,1)} %self_query.1, bf16[8,8192]{1,0:T(8,128)(2,1)} %new_key.1, bf16[8,8192]{1,0:T(8,128)(2,1)} %new_value.1, bf16[8,64,8192]{2,1,0:T(8,128)(2,1)} %cache_keys.1, bf16[8,64,8192]{2,1,0:T(8,128)(2,1)} %cache_values.1, ...), custom_call_target="tpu_custom_call" | custom-call | tf_op jit(solution)/shard_map/pallas_call | solution.py:405
  22.8 1.3 %fusion = (bf16[8,512]{1,0:T(8,128)(2,1)}, bf16[8,512]{1,0:T(8,128)(2,1)}) fusion(bf16[16,512]{1,0:T(8,128)(2,1)} %shard_map.113), kind=kLoop, calls=%fused_computation | loop fusion | bytes 32768 | tf_op jit(solution)/shard_map/slice | solution.py:451
where the time goes:
time: 24.3 us; the launch traced here: 24.1 us
  Pallas kernels  22.2 us (91%)
  local copies, waits for them, and re-layouts  1.32 us (5%)
  between operations  0.64 us (3%)
    pallas_call x1, Pallas kernels, on_device(): pl.pallas_call(functools.partial(kernel, parts, ahead), out_shape=jax.Sha...  22.2 us
    slice x1, local copies, waits for them, and re-layouts, on_device(): return (out[:rows], out[rows:])  1.32 us

commit v1 on v0

v1 whole, which is shorter than its diff:
```python
import functools

import jax
import jax.numpy as jnp
from jax import lax
from jax.experimental import pallas as pl
from jax.experimental.pallas import tpu as pltpu
from jax.sharding import PartitionSpec as P

DH = 128
NEG = -1e30
FLOOR = -1e29
MESH = pl.DeviceIdType.MESH


def mirrored(index, flip, count):
    if count & (count - 1):
        return lax.rem(index + flip, count)
    result, bit = 0, 1
    while bit < count:
        digit = lax.rem(index // bit, 2)
        result = result + bit * (1 - digit if flip & bit else digit)
        bit *= 2
    return result


def kernel(
    parts,
    gather,
    loads,
    ahead,
    plan,
    lengths_in,
    ids_in,
    self_query,
    new_key,
    new_value,
    cache_keys,
    cache_values,
    db_keys,
    db_values,
    cross_query,
    out,
    lengths,
    ids,
    keys,
    values,
    dkeys,
    dvalues,
    squery,
    cquery,
    nkey,
    nvalue,
    marks,
    bias,
    cbias,
    ccounts,
    scores,
    cscores,
    outbox,
    sidebox,
    merged,
    inbox,
    stats,
    stream_sem,
    small_sem,
    send_sem,
    recv_sem,
    side_send,
    side_recv,
):
    me = lax.axis_index("seq")
    rows, positions, width = cache_keys.shape
    entries, tokens, _ = db_keys.shape
    extent = entries * tokens
    span = width // parts
    heads = span // DH
    pairs = heads // 2
    pair_rows = 2 * rows
    groups = parts // gather
    members = gather // 2
    chips = parts // 2
    total = gather * heads * rows
    copies = DH // positions
    chunks = rows // copies

    core = lax.rem(me, 2)
    chip = me // 2
    partner = chip * 2 + 1 - core
    member = lax.rem(chip, members)
    group = chip // members

    def group_at(turn):
        return mirrored(group, groups - 1 - turn, groups)

    def member_at(place):
        return lax.rem(member + 1 + place, members)

    def peer(turn, place):
        return (group_at(turn) * members + member_at(place)) * 2 + core

    def lanes_of(device):
        return pl.ds(pl.multiple_of(device * span, span), span)

    def owner(turn, slot):
        return peer(turn, slot // 2) - core + (core if slot % 2 else 1 - core)

    def stream(kind, turn, slots):
        source, dest = (
            (cache_keys, keys),
            (cache_values, values),
            (db_keys, dkeys),
            (db_values, dvalues),
        )[kind]
        return [
            pltpu.make_async_copy(
                source.at[:, :, lanes_of(owner(turn, s))],
                dest.at[turn, s],
                stream_sem.at[kind, turn, s],
            )
            for s in slots
        ]

    def handover(turn, place):
        step = turn * members + place
        return pltpu.make_async_remote_copy(
            src_ref=outbox.at[turn, 2 * place],
            dst_ref=sidebox.at[step],
            send_sem=side_send.at[step],
            recv_sem=side_recv.at[step],
            device_id={"seq": partner},
            device_id_type=MESH,
        )

    def message(turn, place):
        step = turn * members + place
        return pltpu.make_async_remote_copy(
            src_ref=merged.at[step],
            dst_ref=inbox.at[step],
            send_sem=send_sem.at[step],
            recv_sem=recv_sem.at[step],
            device_id={"seq": peer(turn, place)},
            device_id_type=MESH,
        )

    steps = [(turn, place) for turn in range(groups) for place in range(members)]

    own = lanes_of(me)
    small = [
        pltpu.make_async_copy(self_query, squery, small_sem.at[0]),
        pltpu.make_async_copy(cross_query, cquery, small_sem.at[1]),
        pltpu.make_async_copy(new_key.at[:, own], nkey, small_sem.at[2]),
        pltpu.make_async_copy(new_value.at[:, own], nvalue, small_sem.at[3]),
    ]
    scalars = [
        pltpu.make_async_copy(lengths_in, lengths, small_sem.at[4]),
        pltpu.make_async_copy(ids_in, ids, small_sem.at[5]),
    ]
    everything = range(gather)
    queue = []
    for name in loads:
        turn = int(name[1])
        slots = everything if len(name) == 2 else (2 * int(name[2]), 2 * int(name[2]) + 1)
        for kind in (0, 2) if name[0] == "K" else (1, 3):
            queue.append((kind, turn, slots))

    def launch(count):
        for _ in range(count):
            if queue:
                for copy in stream(*queue.pop(0)):
                    copy.start()

    small[0].start()
    launch(1)
    small[1].start()
    launch(1)
    barrier = pltpu.get_barrier_semaphore()
    for turn, place in steps[:-1]:
        pl.semaphore_signal(
            barrier, inc=1, device_id={"seq": peer(turn, place)}, device_id_type=MESH
        )
    pl.semaphore_signal(barrier, inc=1, device_id={"seq": partner}, device_id_type=MESH)

    for copy in scalars:
        copy.start()
    launch(ahead)
    small[2].start()
    small[3].start()
    tag = lax.broadcasted_iota(jnp.int32, (pair_rows, DH), 1)
    zero = jnp.zeros((rows, DH), jnp.float32)

    def prepare():
        line = lax.rem(lax.broadcasted_iota(jnp.int32, (pair_rows, DH), 0), rows)
        for j in range(chunks):
            mark = jnp.where(line == j * copies + tag // positions, 1.0, 0.0)
            marks[:, j * DH : (j + 1) * DH] = mark.astype(jnp.bfloat16)
        for copy in scalars:
            copy.wait()
        shape = (rows, DH)
        row = lax.broadcasted_iota(jnp.int32, shape, 0)
        spot = lax.rem(lax.broadcasted_iota(jnp.int32, shape, 1), positions)
        table = jnp.full(shape, NEG, jnp.float32)
        for b in range(rows):
            live = (row == b) & (spot < lengths[b] - me * positions)
            table = jnp.where(live, 0.0, table)
        bias[...] = table
        shape = (rows, extent)
        row = lax.broadcasted_iota(jnp.int32, shape, 0)
        lane = lax.broadcasted_iota(jnp.int32, shape, 1)
        table = jnp.zeros(shape, jnp.float32)
        for b in range(rows):
            for e in range(entries):
                here = (row == b) & (lane >= e * tokens) & (lane < (e + 1) * tokens)
                for j in range(ids.shape[0]):
                    match = here & (jnp.full(shape, ids[j, b], jnp.int32) == me * entries + e)
                    table = jnp.where(match, table + 1.0, table)
        ccounts[...] = table
        cbias[...] = jnp.where(table > 0.0, 0.0, NEG)

    def quads_of(source, turn, slot):
        block = source[:, lanes_of(owner(turn, slot))].astype(jnp.float32)
        found = []
        for pair in range(pairs):
            first = block[:, 2 * pair * DH : (2 * pair + 1) * DH]
            second = block[:, (2 * pair + 1) * DH : (2 * pair + 2) * DH]
            quad = jnp.concatenate(
                [
                    jnp.concatenate([first, zero], axis=1),
                    jnp.concatenate([zero, second], axis=1),
                ],
                axis=0,
            )
            found.append(quad.astype(jnp.bfloat16))
        return found

    def piece_of(pair):
        return slice(pair * 2 * DH, (pair + 1) * 2 * DH)

    def score(turn):
        blank = jnp.zeros((pair_rows, 2 * DH), jnp.bfloat16)
        found = None
        for s in range(gather):
            for pair, quad in enumerate(quads_of(squery, turn, s)):
                at = s * pairs + pair
                query = jnp.concatenate(
                    [quad if i == at else blank for i in range(gather * pairs)], axis=0
                )
                held = keys[turn, s, :, :, piece_of(pair)].reshape(rows * positions, 2 * DH)
                part = lax.dot_general(
                    held, query, (((1,), (1,)), ((), ())), preferred_element_type=jnp.float32
                )
                found = part if found is None else found + part
        column = lax.rem(lax.broadcasted_iota(jnp.int32, (positions, total), 1), rows)
        folded = found[:positions]
        for b in range(1, rows):
            folded = jnp.where(column == b, found[b * positions : (b + 1) * positions], folded)
        folded = jnp.concatenate([folded] * copies, axis=0)
        scores[turn % 2] = folded.T

    def cross_score(turn):
        for s in range(gather):
            for pair, quad in enumerate(quads_of(cquery, turn, s)):
                at = s * pairs + pair
                held = dkeys[turn, s, :, :, piece_of(pair)].reshape(extent, 2 * DH)
                cscores[turn % 2, at * pair_rows : (at + 1) * pair_rows] = lax.dot_general(
                    quad,
                    held,
                    (((1,), (1,)), ((), ())),
                    preferred_element_type=jnp.float32,
                )

    def weigh(found, table, number, share):
        depth = found.shape[1]
        level = found.reshape(total // rows, rows, depth) * (DH ** (-0.5)) + table[None]
        peak = jnp.maximum(jnp.max(level, axis=2, keepdims=True), FLOOR)
        weights = jnp.exp(level - peak)
        if number is not None:
            weights = weights * number[None]
        den = jnp.maximum(jnp.sum(weights, axis=2, keepdims=True) * share, 0.5)
        inverse, level = 1.0 / den, peak + jnp.log(den)
        return (
            weights.reshape(total, depth).astype(jnp.bfloat16),
            inverse.reshape(total, 1),
            level.reshape(total, 1),
        )

    def weigh_both(turn):
        return (
            weigh(scores[turn % 2], bias[...], None, 1.0 / copies),
            weigh(cscores[turn % 2], cbias[...], ccounts[...], 1.0),
        )

    def combine(turn, slots, found):
        (weights, inverse, level), (cweights, cinverse, clevel) = found
        for s in slots:
            tile = jnp.zeros((pair_rows, DH), jnp.float32)
            for pair in range(pairs):
                at = (s * pairs + pair) * pair_rows
                mine = slice(at, at + pair_rows)
                expanded = jnp.concatenate([weights[mine]] * chunks, axis=1) * marks[...]
                acc = jnp.dot(
                    expanded,
                    values[turn, s, :, :, piece_of(pair)].reshape(rows * positions, 2 * DH),
                    preferred_element_type=jnp.float32,
                )
                cacc = jnp.dot(
                    cweights[mine],
                    dvalues[turn, s, :, :, piece_of(pair)].reshape(extent, 2 * DH),
                    preferred_element_type=jnp.float32,
                )
                for h in range(2):
                    these = slice(h * rows, (h + 1) * rows)
                    rest = slice(h * DH, (h + 1) * DH)
                    at_head = slice(at + h * rows, at + (h + 1) * rows)
                    part = jnp.concatenate(
                        [
                            acc[these, rest] * inverse[at_head],
                            cacc[these, rest] * cinverse[at_head],
                        ],
                        axis=0,
                    )
                    head = 2 * pair + h
                    outbox[turn, s, :, head * DH : (head + 1) * DH] = part.astype(jnp.bfloat16)
                    both = jnp.concatenate([level[at_head], clevel[at_head]], axis=0)
                    tile = jnp.where(lax.rem(tag, heads) == head, both, tile)
            outbox[turn, s, :, span:] = packed(tile)

    def spread(tile, head):
        return jnp.broadcast_to(tile[:, head : head + 1], (pair_rows, DH))

    def level_of(box):
        raw = box[:, span:].astype(jnp.float32)
        full = raw + pltpu.roll(raw, DH - heads, 1) + pltpu.roll(raw, DH - 2 * heads, 1)
        return jnp.where(tag < heads, full, NEG)

    def packed(level):
        high = level.astype(jnp.bfloat16).astype(jnp.float32)
        rest = level - high
        middle = rest.astype(jnp.bfloat16).astype(jnp.float32)
        low = rest - middle
        level = jnp.where(tag < heads, high, jnp.where(tag < 2 * heads, middle, low))
        return level.astype(jnp.bfloat16)

    def kept(turn, place):
        return outbox.at[turn, 2 * place + 1]

    def merge(turn, place):
        step = turn * members + place
        mine, other_box = kept(turn, place), sidebox.at[step]
        first, second = level_of(mine), level_of(other_box)
        top = jnp.maximum(first, second)
        share, other = jnp.exp(first - top), jnp.exp(second - top)
        both = share + other
        inverse = 1.0 / both
        share, other = share * inverse, other * inverse
        for h in range(heads):
            piece = slice(h * DH, (h + 1) * DH)
            part = mine[:, piece].astype(jnp.float32) * spread(share, h)
            part = part + other_box[:, piece].astype(jnp.float32) * spread(other, h)
            merged[step, :, piece] = part.astype(jnp.bfloat16)
        level = top + jnp.log(both)
        level = jnp.where(tag < heads, level, 0.0)
        level = (
            level
            + jnp.where(tag < 2 * heads, pltpu.roll(level, heads, 1), 0.0)
            + pltpu.roll(level, 2 * heads, 1)
        )
        merged[step, :, span:] = packed(level)

    def arrive(name):
        turn = int(name[1])
        slots = everything if len(name) == 2 else (2 * int(name[2]), 2 * int(name[2]) + 1)
        for kind in (0, 2) if name[0] == "K" else (1, 3):
            for copy in stream(kind, turn, slots):
                copy.wait()

    held = {}

    def run(action):
        name, turn = action[0], int(action[1:2] or 0)
        places = [int(action[2])] if len(action) > 2 else range(members)
        if name == "Q":
            small[turn].wait()
        if name == "M":
            prepare()
        if name in "KV":
            arrive(action)
        if name == "+":
            launch(turn)
        if name == "S":
            score(turn)
            cross_score(turn)
        if name == "W":
            held[turn] = weigh_both(turn)
        if name == "C":
            if turn not in held:
                held[turn] = weigh_both(turn)
            combine(turn, [2 * p + c for p in places for c in range(2)], held[turn])
        if name == "B":
            pl.semaphore_wait(barrier, chips)
        if name == "H":
            for place in places:
                handover(turn, place).start()
        if name == "P":
            for place in places:
                if (turn, place) != steps[-1]:
                    handover(turn, place).wait_recv()
                    merge(turn, place)
                    message(turn, place).start()

    for action in plan:
        run(action)

    small[2].wait()
    small[3].wait()
    query_own = squery[:, own].astype(jnp.float32)
    product = query_own * nkey[...].astype(jnp.float32)
    level_own = jnp.full((rows, DH), NEG, jnp.float32)
    short = tag[:rows]
    for h in range(heads):
        value = jnp.sum(product[:, h * DH : (h + 1) * DH], axis=1, keepdims=True) * (DH ** (-0.5))
        level_own = jnp.where(short == h, value, level_own)
    level_own = jnp.concatenate([level_own, jnp.full((rows, DH), NEG, jnp.float32)], axis=0)

    last = steps[-1]
    boxes = [(kept(*last), None)]
    boxes += [(inbox.at[k], message(*step)) for k, step in enumerate(steps[:-1])]
    boxes.insert(len(boxes) - 1, (sidebox.at[len(steps) - 1], handover(*last)))
    top = level_own
    for k, (box, copy) in enumerate(boxes):
        if copy is not None:
            copy.wait_recv()
        level = level_of(box)
        stats[k] = level
        top = jnp.maximum(top, level)
    share = jnp.exp(level_own - top)
    both = share
    sums = [
        jnp.concatenate([nvalue[:, h * DH : (h + 1) * DH].astype(jnp.float32), zero], axis=0)
        * spread(share, h)
        for h in range(heads)
    ]
    for k, (box, _) in enumerate(boxes):
        share = jnp.exp(stats[k] - top)
        both = both + share
        for h in range(heads):
            part = box[:, h * DH : (h + 1) * DH].astype(jnp.float32)
            sums[h] = sums[h] + part * spread(share, h)
    inverse = 1.0 / both
    for h in range(heads):
        result = sums[h] * spread(inverse, h)
        out[:, h * DH : (h + 1) * DH] = result.astype(jnp.bfloat16)

    for step in steps[:-1]:
        message(*step).wait_send()
    for step in steps:
        handover(*step).wait_send()


def on_device(
    self_query,
    new_key,
    new_value,
    cache_keys,
    cache_values,
    lengths,
    db_keys,
    db_values,
    cross_query,
    neighbour_ids,
):
    parts = lax.axis_size("seq")
    rows, positions, width = cache_keys.shape
    entries, tokens, _ = db_keys.shape
    span = width // parts
    chips = parts // 2
    gather = min(parts, DH * DH // (span * rows))
    groups = parts // gather
    total = gather * span // DH * rows
    half = jnp.bfloat16
    anywhere = pl.BlockSpec(memory_space=pl.ANY)
    vmem = pl.BlockSpec(memory_space=pltpu.VMEM)
    box = (2 * rows, span + DH)
    out = pl.pallas_call(
        functools.partial(kernel, parts, gather, ['K0', 'V0', 'K1', 'V1', 'K2', 'V2', 'K3', 'V30', 'V31'], 4, ['Q0', 'K0', '+2', 'Q1', 'S0', 'V0', '+2', 'M', 'C0', 'K1', '+9', '+9', 'S1', 'B', 'H0', 'V1', 'K2', 'S2', 'C1', 'P0', 'H1', 'V2', 'K3', 'S3', 'C2', 'P1', 'H2', 'V30', 'C30', 'H30', 'P2', 'V31', 'C31', 'H31', 'P30']),
        out_shape=pltpu.VMEM((2 * rows, span), half),
        in_specs=[anywhere] * 10,
        out_specs=vmem,
        scratch_shapes=[
            pltpu.SMEM(lengths.shape, jnp.int32),
            pltpu.SMEM(neighbour_ids.shape[::-1], jnp.int32),
            pltpu.VMEM((groups, gather, rows, positions, span), half),
            pltpu.VMEM((groups, gather, rows, positions, span), half),
            pltpu.VMEM((groups, gather, entries, tokens, span), half),
            pltpu.VMEM((groups, gather, entries, tokens, span), half),
            pltpu.VMEM((rows, width), half),
            pltpu.VMEM((rows, width), half),
            pltpu.VMEM((rows, span), half),
            pltpu.VMEM((rows, span), half),
            pltpu.VMEM((2 * rows, rows * positions), half),
            pltpu.VMEM((rows, DH), jnp.float32),
            pltpu.VMEM((rows, entries * tokens), jnp.float32),
            pltpu.VMEM((rows, entries * tokens), jnp.float32),
            pltpu.VMEM((2, total, DH), jnp.float32),
            pltpu.VMEM((2, total, entries * tokens), jnp.float32),
            pltpu.VMEM((groups, gather, *box), half),
            pltpu.VMEM((chips, *box), half),
            pltpu.VMEM((chips, *box), half),
            pltpu.VMEM((chips, *box), half),
            pltpu.VMEM((chips + 1, 2 * rows, DH), jnp.float32),
            pltpu.SemaphoreType.DMA((4, groups, gather)),
            pltpu.SemaphoreType.DMA((6,)),
            pltpu.SemaphoreType.DMA((chips,)),
            pltpu.SemaphoreType.DMA((chips,)),
            pltpu.SemaphoreType.DMA((chips,)),
            pltpu.SemaphoreType.DMA((chips,)),
        ],
        compiler_params=pltpu.CompilerParams(
            collective_id=0, has_side_effects=True, vmem_limit_bytes=48 * 1024 * 1024
        ),
    )(
        *[
            pltpu.with_memory_space_constraint(array, pltpu.HBM)
            for array in (
                lengths,
                neighbour_ids.T,
                self_query,
                new_key,
                new_value,
                cache_keys,
                cache_values,
                db_keys,
                db_values,
                cross_query,
            )
        ]
    )
    return out[:rows], out[rows:]


def solution(mesh):
    in_specs = (
        P("groups", None),
        P("groups", None),
        P("groups", None),
        P("groups", "seq", None),
        P("groups", "seq", None),
        P("groups"),
        P(("groups", "seq"), None, None),
        P(("groups", "seq"), None, None),
        P("groups", None),
        P("groups", None),
    )
    out_specs = (P("groups", "seq"), P("groups", "seq"))
    return jax.shard_map(
        on_device, mesh=mesh, in_specs=in_specs, out_specs=out_specs, check_vma=False
    )
```

time: 24.3 us -> 19 us (0.78)
  Pallas kernels: 22.2 us -> 17.6 us
  local copies, waits for them, and re-layouts: 1.32 us -> 0.61 us
    pallas_call x1, Pallas kernels: 22.2 us -> 17.6 us  [on_device(): pl.pallas_call(functools.partial(kernel, parts, gather, ['K0', 'V0', 'K1'...]
    slice x1, local copies, waits for them, and re-layouts: 1.32 us -> 0.61 us  [on_device(): return (out[:rows], out[rows:])]
where the time goes in v1:
time: 19 us; the launch traced here: 18.8 us
  Pallas kernels  17.6 us (93%)
  between operations  0.64 us (3%)
  local copies, waits for them, and re-layouts  0.61 us (3%)
    pallas_call x1, Pallas kernels, on_device(): pl.pallas_call(functools.partial(kernel, parts, gather, ['K0', 'V0', 'K1'...  17.6 us
    slice x1, local copies, waits for them, and re-layouts, on_device(): return (out[:rows], out[rows:])  0.61 us

profile of v1, /device:TPU:0, one launch (start us, length us, event | category | flops | bytes accessed | tf_op | source)
XLA Modules:
  0.0 18.8 jit_solution(12857257858950819214)
XLA Ops:
  0.6 17.6 %shard_map.113 = bf16[16,512]{1,0:T(8,128)(2,1)S(1)} custom-call(s32[8]{0:T(128)} %lengths_in.1, s32[2,8]{1,0:T(2,128)} %bitcast.1, bf16[8,8192]{1,0:T(8,128)(2,1)} %self_query.1, bf16[8,8192]{1,0:T(8,128)(2,1)} %new_key.1, bf16[8,8192]{1,0:T(8,128)(2,1)} %new_value.1, bf16[8,64,8192]{2,1,0:T(8,128)(2,1)} %cache_keys.1, bf16[8,64,8192]{2,1,0:T(8,128)(2,1)} %cache_values.1, ...), custom_call_target="tpu_custom_call" | custom-call | tf_op jit(solution)/shard_map/pallas_call | solution.py:484
  18.2 0.6 %fusion = (bf16[8,512]{1,0:T(8,128)(2,1)}, bf16[8,512]{1,0:T(8,128)(2,1)}) fusion(bf16[16,512]{1,0:T(8,128)(2,1)S(1)} %shard_map.113), kind=kLoop, calls=%fused_computation | loop fusion | bytes 32768 | tf_op jit(solution)/shard_map/slice | solution.py:538

commit v2 on v1

--- a/solution.py
+++ b/solution.py
@@ -61,7 +61,6 @@
     sidebox,
     merged,
     inbox,
-    stats,
     stream_sem,
     small_sem,
     send_sem,
@@ -171,9 +170,8 @@
                     copy.start()
 
     small[0].start()
-    launch(1)
     small[1].start()
-    launch(1)
+    launch(2)
     barrier = pltpu.get_barrier_semaphore()
     for turn, place in steps[:-1]:
         pl.semaphore_signal(
@@ -236,10 +234,12 @@
     def piece_of(pair):
         return slice(pair * 2 * DH, (pair + 1) * 2 * DH)
 
-    def score(turn):
+    def score(turn, staged=False):
         blank = jnp.zeros((pair_rows, 2 * DH), jnp.bfloat16)
         found = None
         for s in range(gather):
+            if staged:
+                stream(0, turn, [s])[0].wait()
             for pair, quad in enumerate(quads_of(squery, turn, s)):
                 at = s * pairs + pair
                 query = jnp.concatenate(
@@ -258,16 +258,25 @@
         scores[turn % 2] = folded.T
 
     def cross_score(turn):
-        for s in range(gather):
-            for pair, quad in enumerate(quads_of(cquery, turn, s)):
-                at = s * pairs + pair
-                held = dkeys[turn, s, :, :, piece_of(pair)].reshape(extent, 2 * DH)
-                cscores[turn % 2, at * pair_rows : (at + 1) * pair_rows] = lax.dot_general(
-                    quad,
-                    held,
+        count = gather * pairs
+        batch = min(4, count)
+        blank = jnp.zeros((pair_rows, 2 * DH), jnp.bfloat16)
+        quads = sum((quads_of(cquery, turn, s) for s in range(gather)), [])
+        for start in range(0, count, batch):
+            found = None
+            for at in range(start, start + batch):
+                query = jnp.concatenate(
+                    [quads[at] if i == at else blank for i in range(start, start + batch)], axis=0
+                )
+                held = dkeys[turn, at // pairs, :, :, piece_of(at % pairs)]
+                part = lax.dot_general(
+                    held.reshape(extent, 2 * DH),
+                    query,
                     (((1,), (1,)), ((), ())),
                     preferred_element_type=jnp.float32,
                 )
+                found = part if found is None else found + part
+            cscores[turn % 2, start * pair_rows : (start + batch) * pair_rows] = found.T
 
     def weigh(found, table, number, share):
         depth = found.shape[1]
@@ -387,6 +396,9 @@
             arrive(action)
         if name == "+":
             launch(turn)
+        if name == "Z":
+            score(turn, True)
+            cross_score(turn)
         if name == "S":
             score(turn)
             cross_score(turn)
@@ -402,11 +414,13 @@
             for place in places:
                 handover(turn, place).start()
         if name == "P":
-            for place in places:
-                if (turn, place) != steps[-1]:
-                    handover(turn, place).wait_recv()
-                    merge(turn, place)
-                    message(turn, place).start()
+            outgoing = [place for place in places if (turn, place) != steps[-1]]
+            for place in outgoing:
+                handover(turn, place).wait_recv()
+            for place in outgoing:
+                merge(turn, place)
+            for place in outgoing:
+                message(turn, place).start()
 
     for action in plan:
         run(action)
@@ -423,33 +437,40 @@
     level_own = jnp.concatenate([level_own, jnp.full((rows, DH), NEG, jnp.float32)], axis=0)
 
     last = steps[-1]
-    boxes = [(kept(*last), None)]
-    boxes += [(inbox.at[k], message(*step)) for k, step in enumerate(steps[:-1])]
-    boxes.insert(len(boxes) - 1, (sidebox.at[len(steps) - 1], handover(*last)))
-    top = level_own
-    for k, (box, copy) in enumerate(boxes):
-        if copy is not None:
-            copy.wait_recv()
-        level = level_of(box)
-        stats[k] = level
-        top = jnp.maximum(top, level)
-    share = jnp.exp(level_own - top)
-    both = share
+    waves = [
+        [(kept(*last), None), (sidebox.at[len(steps) - 1], handover(*last))],
+        [(inbox.at[k], message(*step)) for k, step in enumerate(steps[:-1])],
+    ]
+
+    def fold(top, both, sums, boxes):
+        for _, copy in boxes:
+            if copy is not None:
+                copy.wait_recv()
+        levels = [level_of(box) for box, _ in boxes]
+        peak = functools.reduce(jnp.maximum, levels, top)
+        shares = [jnp.exp(level - peak) for level in levels]
+        scale = both * jnp.exp(top - peak)
+        both = functools.reduce(jnp.add, shares, scale)
+        inverse = 1.0 / both
+        shares = [share * inverse for share in shares]
+        scale = scale * inverse
+        for h in range(heads):
+            result = sums[h] * spread(scale, h)
+            for share, (box, _) in zip(shares, boxes):
+                part = box[:, h * DH : (h + 1) * DH].astype(jnp.float32)
+                result = result + part * spread(share, h)
+            sums[h] = result
+        return peak, both, sums
+
     sums = [
         jnp.concatenate([nvalue[:, h * DH : (h + 1) * DH].astype(jnp.float32), zero], axis=0)
-        * spread(share, h)
         for h in range(heads)
     ]
-    for k, (box, _) in enumerate(boxes):
-        share = jnp.exp(stats[k] - top)
-        both = both + share
-        for h in range(heads):
-            part = box[:, h * DH : (h + 1) * DH].astype(jnp.float32)
-            sums[h] = sums[h] + part * spread(share, h)
-    inverse = 1.0 / both
+    top, both = level_own, jnp.ones((pair_rows, DH), jnp.float32)
+    for wave in waves:
+        top, both, sums = fold(top, both, sums, wave)
     for h in range(heads):
-        result = sums[h] * spread(inverse, h)
-        out[:, h * DH : (h + 1) * DH] = result.astype(jnp.bfloat16)
+        out[:, h * DH : (h + 1) * DH] = sums[h].astype(jnp.bfloat16)
 
     for step in steps[:-1]:
         message(*step).wait_send()
@@ -482,7 +503,7 @@
     vmem = pl.BlockSpec(memory_space=pltpu.VMEM)
     box = (2 * rows, span + DH)
     out = pl.pallas_call(
-        functools.partial(kernel, parts, gather, ['K0', 'V0', 'K1', 'V1', 'K2', 'V2', 'K3', 'V30', 'V31'], 4, ['Q0', 'K0', '+2', 'Q1', 'S0', 'V0', '+2', 'M', 'C0', 'K1', '+9', '+9', 'S1', 'B', 'H0', 'V1', 'K2', 'S2', 'C1', 'P0', 'H1', 'V2', 'K3', 'S3', 'C2', 'P1', 'H2', 'V30', 'C30', 'H30', 'P2', 'V31', 'C31', 'H31', 'P30']),
+        functools.partial(kernel, parts, gather, ['K0', 'K1', 'V0', 'K2', 'V1', 'K3', 'V2', 'V30', 'V31'], 8, ['Q0', 'K0', '+2', 'Q1', 'M', 'S0', 'K1', 'V0', '+9', '+9', 'S1', 'C0', 'B', 'H0', 'V1', 'K2', 'S2', 'C1', 'P0', 'H1', 'V2', 'K3', 'S3', 'C2', 'P1', 'H2', 'V30', 'C30', 'H30', 'P2', 'V31', 'C31', 'H31', 'P30']),
         out_shape=pltpu.VMEM((2 * rows, span), half),
         in_specs=[anywhere] * 10,
         out_specs=vmem,
@@ -507,7 +528,6 @@
             pltpu.VMEM((chips, *box), half),
             pltpu.VMEM((chips, *box), half),
             pltpu.VMEM((chips, *box), half),
-            pltpu.VMEM((chips + 1, 2 * rows, DH), jnp.float32),
             pltpu.SemaphoreType.DMA((4, groups, gather)),
             pltpu.SemaphoreType.DMA((6,)),
             pltpu.SemaphoreType.DMA((chips,)),

time: 19 us -> 18.1 us (0.953)
  Pallas kernels: 17.6 us -> 16.7 us
    pallas_call x1, Pallas kernels: 17.6 us -> 16.7 us  [on_device(): pl.pallas_call(functools.partial(kernel, parts, gather, ['K0', 'K1', 'V0'...]
where the time goes in v2:
time: 18.1 us; the launch traced here: 17.9 us
  Pallas kernels  16.7 us (92%)
  between operations  0.64 us (4%)
  local copies, waits for them, and re-layouts  0.61 us (3%)
    pallas_call x1, Pallas kernels, on_device(): pl.pallas_call(functools.partial(kernel, parts, gather, ['K0', 'K1', 'V0'...  16.7 us
    slice x1, local copies, waits for them, and re-layouts, on_device(): return (out[:rows], out[rows:])  0.61 us

profile of v2, /device:TPU:0, one launch (start us, length us, event | category | flops | bytes accessed | tf_op | source)
XLA Modules:
  0.0 17.9 jit_solution(7907854754607821366)
XLA Ops:
  0.6 16.7 %shard_map.113 = bf16[16,512]{1,0:T(8,128)(2,1)S(1)} custom-call(s32[8]{0:T(128)} %lengths_in.1, s32[2,8]{1,0:T(2,128)} %bitcast.1, bf16[8,8192]{1,0:T(8,128)(2,1)} %self_query.1, bf16[8,8192]{1,0:T(8,128)(2,1)} %new_key.1, bf16[8,8192]{1,0:T(8,128)(2,1)} %new_value.1, bf16[8,64,8192]{2,1,0:T(8,128)(2,1)} %cache_keys.1, bf16[8,64,8192]{2,1,0:T(8,128)(2,1)} %cache_values.1, ...), custom_call_target="tpu_custom_call" | custom-call | tf_op jit(solution)/shard_map/pallas_call | solution.py:505
  17.3 0.6 %fusion = (bf16[8,512]{1,0:T(8,128)(2,1)}, bf16[8,512]{1,0:T(8,128)(2,1)}) fusion(bf16[16,512]{1,0:T(8,128)(2,1)S(1)} %shard_map.113), kind=kLoop, calls=%fused_computation | loop fusion | bytes 32768 | tf_op jit(solution)/shard_map/slice | solution.py:558
